TPU v7x, 32 devices: a whole 2x2x4 slice. The times are simulated.
32 devices in a mesh: band: 8 (over z, y), grid: 4 (over x, core).
Axes of the slice: x: 2, y: 2, z: 4, core: 2. Of those that a mesh axis runs over, the one named last changes fastest.
Arguments:
- orbitals: bfloat16 [8, 128, 128, 128], P('band', 'grid'), may hold values from -3 to 3
- trial_vectors: bfloat16 [2, 8, 128, 128, 128], P(None, 'band', 'grid'), may hold values from -6 to 6
- alda_kernel: float32 [128, 128, 128], P('grid'), may hold values from -2 to -0.5
- local_potential: float32 [128, 128, 128], P('grid'), may hold values from -2 to 1
- band_energies: float32 [8], P('band'), may hold values from -1.5 to -0.2
Outputs:
- sigma_real: float32 [2, 8, 128, 128, 128], P(None, 'band', 'grid')
- sigma_imag: float32 [2, 8, 128, 128, 128], P(None, 'band', 'grid')
All inputs are finite; a program needn't handle non-finite values.
Results may differ from a plain program's by a relative error of at most 0.0003.
Values sent between devices are 32-bit elements; how exact they have to be, the bound alone decides.
A program may use at most 64 MiB of HBM per device.

v0:
```python
import math
import jax
import jax.numpy as jnp
from jax import lax
from jax.sharding import PartitionSpec as P

box_length = 30.0
highest = lax.Precision.HIGHEST


def tables(length):
    positions = jnp.arange(length, dtype=jnp.int32)
    wrapped = positions[:, None] * positions[None, :] % length
    angles = wrapped.astype(jnp.float32) * (2.0 * math.pi / length)
    return (jnp.cos(angles), jnp.sin(angles))


def contract(pattern, left_operand, right_operand):
    return jnp.einsum(pattern, left_operand, right_operand, precision=highest)


def rotate(pattern, real_part, imag_part, cosine_table, sine_table, orient):
    new_real = contract(pattern, real_part, cosine_table) - orient * contract(
        pattern, imag_part, sine_table
    )
    new_imag = contract(pattern, imag_part, cosine_table) + orient * contract(
        pattern, real_part, sine_table
    )
    return (new_real, new_imag)


def rotate_real(pattern, real_part, cosine_table, sine_table, orient):
    return (
        contract(pattern, real_part, cosine_table),
        orient * contract(pattern, real_part, sine_table),
    )


def frequency(length, offset, extent):
    positions = offset + jnp.arange(extent, dtype=jnp.int32)
    signed = jnp.where(2 * positions < length, positions, positions - length)
    return signed.astype(jnp.float32)


def coulomb(first_freq, second_freq, third_freq):
    squared = (
        first_freq[:, None, None] ** 2
        + second_freq[None, :, None] ** 2
        + third_freq[None, None, :] ** 2
    )
    scaled = box_length**2 / math.pi / jnp.maximum(squared, 1.0)
    return jnp.where(squared > 0, scaled, 0.0)


def potential_split(density_share, cosine_table, sine_table, length):
    real_part, imag_part = rotate_real(
        "kxyz,zg->kxgy", density_share, cosine_table, sine_table, -1.0
    )
    arrived = lax.all_to_all(
        jnp.stack((real_part, imag_part)), "band", split_axis=3, concat_axis=4, tiled=True
    )
    real_part, imag_part = rotate(
        "kxzy,yg->kgzx", arrived[0], arrived[1], cosine_table, sine_table, -1.0
    )
    arrived = lax.all_to_all(
        jnp.stack((real_part, imag_part)), "grid", split_axis=2, concat_axis=4, tiled=True
    )
    real_part, imag_part = rotate(
        "kyzx,xg->kyzg", arrived[0], arrived[1], cosine_table, sine_table, -1.0
    )
    rows_here = real_part.shape[1]
    planes_here = real_part.shape[2]
    kernel = coulomb(
        frequency(length, lax.axis_index("grid") * rows_here, rows_here),
        frequency(length, lax.axis_index("band") * planes_here, planes_here),
        frequency(length, 0, length),
    )
    real_part = real_part * kernel[None]
    imag_part = imag_part * kernel[None]
    real_part, imag_part = rotate(
        "kyzg,gx->kyzx", real_part, imag_part, cosine_table, sine_table, 1.0
    )
    arrived = lax.all_to_all(
        jnp.stack((real_part, imag_part)), "grid", split_axis=4, concat_axis=2, tiled=True
    )
    real_part, imag_part = rotate(
        "kgzx,gy->kxzy", arrived[0], arrived[1], cosine_table, sine_table, 1.0
    )
    arrived = lax.all_to_all(
        jnp.stack((real_part, imag_part)), "band", split_axis=4, concat_axis=3, tiled=True
    )
    restored = contract("kxgy,gz->kxyz", arrived[0], cosine_table) - contract(
        "kxgy,gz->kxyz", arrived[1], sine_table
    )
    return restored / float(length**3)


def per_device(orbitals, trial_vectors, alda_kernel, local_potential, band_energies):
    length = orbitals.shape[2]
    cosine_table, sine_table = tables(length)
    orbital_wide = orbitals.astype(jnp.float32)
    trial_wide = trial_vectors.astype(jnp.float32)
    partial_value = 2.0 * jnp.sum(trial_wide * orbital_wide[None], axis=1)
    density_share = lax.psum_scatter(partial_value, "band", scatter_dimension=2, tiled=True)
    row_count = density_share.shape[2]
    kernel_rows = lax.dynamic_slice_in_dim(
        alda_kernel, lax.axis_index("band") * row_count, row_count, 1
    )
    hartree = potential_split(density_share, cosine_table, sine_table, length)
    potential = lax.all_gather(
        hartree + kernel_rows[None] * density_share, "band", axis=2, tiled=True
    )
    weight = local_potential[None] - band_energies[:, None, None, None]
    fields = potential[:, None] * orbital_wide[None] + weight[None] * trial_wide
    trial_count = trial_vectors.shape[0]
    norm_factor = float(length) ** (-1.5)
    pieces = []
    for trial_index in range(trial_count):
        real_part, imag_part = rotate_real(
            "mxyz,zg->mxyg", fields[trial_index], cosine_table, sine_table, -1.0
        )
        real_part, imag_part = rotate(
            "mxyz,yg->mgzx", real_part, imag_part, cosine_table, sine_table, -1.0
        )
        received = lax.all_to_all(
            jnp.stack((real_part, imag_part)), "grid", split_axis=2, concat_axis=4, tiled=True
        )
        finish_real_part, finish_imag_part = rotate(
            "myzx,xg->myzg", received[0], received[1], cosine_table, sine_table, -1.0
        )
        pieces.append(jnp.stack((finish_real_part * norm_factor, finish_imag_part * norm_factor)))
    results = jnp.stack(pieces, axis=1)
    return (results[0], results[1])


def solution(mesh):
    placed = (
        P("band", "grid", None, None),
        P(None, "band", "grid", None, None),
        P("grid", None, None),
        P("grid", None, None),
        P("band"),
    )
    return jax.shard_map(
        per_device,
        mesh=mesh,
        in_specs=placed,
        out_specs=(P(None, "band", "grid", None, None), P(None, "band", "grid", None, None)),
        check_vma=False,
    )
```

profile of v0, /device:TPU:0, one launch (start us, length us, event | category | flops | bytes accessed | tf_op | source)
XLA Modules:
  0.0 582.9 jit_solution(3529673383581125716)
XLA Ops:
  10.2 2.7 fusion.1
  13.0 91.5 %reduce-scatter.2.cloned.1.call-done = f32[2,32,16,128]{3,2,1,0:T(8,128)} async-done(((f32[2,32,128,128]{3,2,1,0:T(8,128)}), f32[2,32,16,128]{3,2,1,0:T(8,128)}) %reduce-scatter.2.cloned.1.call-update) | async-done | bytes 524304 | tf_op jit(solution)/shard_map/reduce_scatter | solution.py:104
  108.4 4.4 copy.166
  112.8 4.8 reshape.245
  117.6 4.6 all-to-all-start
  122.2 25.6 %all-to-all-done = f32[8,1,32768]{2,1,0:T(1,128)S(1)} async-done(((f32[8,1,32768]{2,1,0:T(1,128)}), f32[8,1,32768]{2,1,0:T(1,128)S(1)}, u32[]{:S(2)}, u32[]{:S(2)}) %all-to-all-start) | async-done | bytes 1048608 | tf_op jit(solution)/shard_map/all_to_all | solution.py:59
  149.4 4.3 reduce
  153.7 3.4 reshape.246
  157.1 2.6 copy.167
  160.4 3.5 convolution_multiply_fusion.1
  164.1 3.5 convolution_multiply_fusion
  167.6 14.0 %fusion.27 = f32[1,2,128,16,32]{2,4,3,1,0:T(8,128)S(1)} fusion(f32[128,2,32,16]{0,2,3,1:T(8,128)S(1)} %convolution_multiply_fusion.1, f32[2,32,16,128]{1,3,2,0:T(8,128)S(1)} %bitcast.275), kind=kOutput, calls=%fused_computation.44 | convolution fusion | flops 201687040 | bytes 1572864 | tf_op jit(solution)/shard_map/kxzy,yg->kgzx/dot_general | solution.py:19
  181.6 3.5 fusion.26
  185.1 4.4 copy.174
  189.5 4.8 reshape.247
  194.4 4.2 all-to-all-start.1
  198.9 14.2 %all-to-all-done.1 = f32[4,1,65536]{2,1,0:T(1,128)} async-done(((f32[4,1,65536]{2,1,0:T(1,128)}), f32[4,1,65536]{2,1,0:T(1,128)}, u32[]{:S(2)}, u32[]{:S(2)}) %all-to-all-start.1) | async-done | bytes 1048608 | tf_op jit(solution)/shard_map/all_to_all | solution.py:65
  213.1 4.6 reduce.1
  217.7 3.5 reshape.248
  221.2 4.9 copy.248
  226.0 2.3 fusion.316
  228.4 2.4 squeeze.38
  230.8 2.8 squeeze.39
  240.4 4.4 copy.176
  244.8 3.9 reshape.249
  248.7 17.7 %all_to_all.90 = f32[4,1,65536]{2,1,0:T(1,128)} all-to-all(f32[4,1,65536]{2,1,0:T(1,128)S(1)} %reshape.249), channel_id=1, replica_groups=mesh['band'=8,'grid'=4] {'grid'}, dimensions={0} | all-to-all | bytes 2097152 | tf_op jit(solution)/shard_map/all_to_all | solution.py:83
  266.4 4.6 reduce.2
  271.0 3.5 reshape.250
  274.5 4.9 copy.247
  279.4 2.3 fusion.315
  281.6 2.4 squeeze.40
  286.5 2.4 squeeze.41
  290.9 4.4 copy.178
  295.3 4.8 reshape.251
  300.2 3.6 all-to-all-start.3
  304.3 25.1 %all-to-all-done.3 = f32[8,1,32768]{2,1,0:T(1,128)S(1)} async-done(((f32[8,1,32768]{2,1,0:T(1,128)}), f32[8,1,32768]{2,1,0:T(1,128)S(1)}, u32[]{:S(2)}, u32[]{:S(2)}) %all-to-all-start.3) | async-done | bytes 1048608 | tf_op jit(solution)/shard_map/all_to_all | solution.py:89
  329.4 3.1 reduce.3
  332.5 3.4 reshape.252
  335.9 4.6 copy.179
  347.7 2.7 fusion.29
  351.1 3.3 broadcast_subtract_fusion
  354.4 69.1 %all-gather.2.cloned.1.call-done = f32[2,32,128,128]{3,2,1,0:T(8,128)} async-done(((f32[2,32,16,128]{3,2,1,0:T(8,128)}), f32[2,32,128,128]{3,2,1,0:T(8,128)}) %all-gather.2.cloned.1.call-update) | async-done | bytes 4194320 | tf_op jit(solution)/shard_map/all_gather | solution.py:110
  423.5 4.7 fusion.2
  436.8 2.3 subtract_bitcast_fusion.1
  439.1 2.7 add_bitcast_fusion.1
  442.3 4.4 copy.188
  446.7 4.8 all-to-all-start.4
  451.6 3.8 fusion.8
  464.2 2.5 add_bitcast_fusion
  467.1 4.4 copy.201
  471.6 28.2 %all-to-all-done.4 = f32[2,1,128,128,32]{3,4,1,0,2:T(8,128)} async-done(((f32[2,1,128,128,32]{3,4,1,0,2:T(8,128)}), f32[2,1,128,128,32]{3,4,1,0,2:T(8,128)}, u32[]{:S(2)}, u32[]{:S(2)}) %all-to-all-start.4) | async-done | bytes 4194336 | tf_op jit(solution)/shard_map/all_to_all | solution.py:125
  499.8 4.9 all-to-all-start.5
  504.6 2.7 copy.189
  508.3 3.6 fusion.92
  511.9 5.0 multiply_bitcast_fusion.3
  517.0 4.0 fusion.90
  521.0 4.9 multiply_bitcast_fusion.2
  525.9 26.9 %all-to-all-done.5 = f32[2,1,128,128,32]{3,4,1,0,2:T(8,128)} async-done(((f32[2,1,128,128,32]{3,4,1,0,2:T(8,128)}), f32[2,1,128,128,32]{3,4,1,0,2:T(8,128)}, u32[]{:S(2)}, u32[]{:S(2)}) %all-to-all-start.5) | async-done | bytes 4194336 | tf_op jit(solution)/shard_map/all_to_all | solution.py:125
  552.8 2.7 copy.202
  556.3 3.6 fusion.87
  560.1 3.8 fusion.85
  563.9 3.7 multiply_bitcast_fusion.1
  567.6 3.6 multiply_bitcast_fusion
  572.2 3.6 fusion.5
  (82 shorter events, 49.3 us)
Async XLA Ops:
  7.2 297.1 %copy-start = (f32[32,128,128]{2,1,0:T(8,128)S(1)}, f32[32,128,128]{2,1,0:T(8,128)}, u32[]{:S(2)}) copy-start(f32[32,128,128]{2,1,0:T(8,128)} %param.7) | copy-start | bytes 6291460
  7.2 97.3 %reduce-scatter.2.cloned.1.call-start = ((), (), s32[]{:S(2)}) async-start(), calls=%async_computation.7 | async-start | bytes 4718592 | tf_op jit(solution)/shard_map/reduce_scatter | solution.py:104
  7.2 3.0 copy-start.6
  8.9 1.4 copy-start.4
  117.6 30.2 %all-to-all-start = ((f32[8,1,32768]{2,1,0:T(1,128)}), f32[8,1,32768]{2,1,0:T(1,128)S(1)}, u32[]{:S(2)}, u32[]{:S(2)}) async-start(f32[8,1,32768]{2,1,0:T(1,128)} %reshape.245), calls=%async_computation.1 | async-start | bytes 2097152 | tf_op jit(solution)/shard_map/all_to_all | solution.py:59
  147.9 1.0 copy-start.10
  194.4 18.7 %all-to-all-start.1 = ((f32[4,1,65536]{2,1,0:T(1,128)}), f32[4,1,65536]{2,1,0:T(1,128)}, u32[]{:S(2)}, u32[]{:S(2)}) async-start(f32[4,1,65536]{2,1,0:T(1,128)} %reshape.247), calls=%async_computation.2 | async-start | bytes 2097152 | tf_op jit(solution)/shard_map/all_to_all | solution.py:65
  289.0 1.7 copy-start.11
  300.2 29.2 %all-to-all-start.3 = ((f32[8,1,32768]{2,1,0:T(1,128)}), f32[8,1,32768]{2,1,0:T(1,128)S(1)}, u32[]{:S(2)}, u32[]{:S(2)}) async-start(f32[8,1,32768]{2,1,0:T(1,128)} %reshape.251), calls=%async_computation.4 | async-start | bytes 2097152 | tf_op jit(solution)/shard_map/all_to_all | solution.py:89
  303.8 119.7 %all-gather.2.cloned.1.call-start = ((), (), s32[]{:S(2)}) async-start(), calls=%async_computation.8 | async-start | bytes 4718592 | tf_op jit(solution)/shard_map/all_gather | solution.py:110
  346.0 1.7 copy-start.9
  351.1 72.4 %copy-start.5 = (f32[32,128,128]{2,1,0:T(8,128)S(1)}, f32[32,128,128]{2,1,0:T(8,128)}, u32[]{:S(2)}) copy-start(f32[32,128,128]{2,1,0:T(8,128)} %copy-done.4) | copy-start | bytes 6291460
  428.2 2.1 copy-start.2
  446.7 53.1 %all-to-all-start.4 = ((f32[2,1,128,128,32]{3,4,1,0,2:T(8,128)}), f32[2,1,128,128,32]{3,4,1,0,2:T(8,128)}, u32[]{:S(2)}, u32[]{:S(2)}) async-start(f32[2,1,128,128,32]{3,4,1,0,2:T(8,128)} %copy.188), calls=%async_computation.5 | async-start | bytes 8388608 | tf_op jit(solution)/shard_map/all_to_all | solution.py:125
  451.6 3.8 copy-start.3
  499.8 53.1 %all-to-all-start.5 = ((f32[2,1,128,128,32]{3,4,1,0,2:T(8,128)}), f32[2,1,128,128,32]{3,4,1,0,2:T(8,128)}, u32[]{:S(2)}, u32[]{:S(2)}) async-start(f32[2,1,128,128,32]{3,4,1,0,2:T(8,128)} %copy.201), calls=%async_computation.6 | async-start | bytes 8388608 | tf_op jit(solution)/shard_map/all_to_all | solution.py:125
  567.6 3.6 copy-start.7
  567.6 3.6 copy-start.8
  572.2 3.6 copy-start.1
Sparse Core Ops, SparseCore 0:
  13.1 91.3 reduce-scatter.1
  350.5 72.9 all-gather.1
where the time goes:
time: 588 us; the launch traced here: 583 us
  waiting for transfers between devices  281 us (48%)
  local copies, waits for them, and re-layouts  108 us (18%)
  matrix products  103 us (18%)
  other arithmetic  35.2 us (6%)
  starting transfers between devices  22.7 us (4%)
  blocking collectives  17.7 us (3%)
  between operations  15.6 us (3%)
    dot_general x36, matrix products, contract(): return jnp.einsum(pattern, left_operand, right_operand, precision=highest)  99 us
    reduce_scatter x1, waiting for transfers between devices, per_device(): lax.psum_scatter(partial_value, 'band', scatter_dimension=2, tiled=True)  91.5 us
    all_gather x1, waiting for transfers between devices, per_device(): lax.all_gather(hartree + kernel_rows[None] * density_share, 'band', axis=...  69.1 us
    all_to_all x2, waiting for transfers between devices, per_device(): lax.all_to_all(jnp.stack((real_part, imag_part)), 'grid', split_axis=2, c...  55.1 us
    unnamed x32, local copies, waits for them, and re-layouts  34.5 us
    all_to_all x1, waiting for transfers between devices, potential_split(): lax.all_to_all(jnp.stack((real_part, imag_part)), 'band', split_axis=3, c...  25.6 us
    all_to_all x1, waiting for transfers between devices, potential_split(): lax.all_to_all(jnp.stack((real_part, imag_part)), 'band', split_axis=4, c...  25.1 us
    all_to_all x1, blocking collectives, potential_split(): lax.all_to_all(jnp.stack((real_part, imag_part)), 'grid', split_axis=4, c...  17.7 us
  transfers between devices with their start and end apart: 7, of which 7 were waited for; matrix products, arithmetic and copies ran while one was open for 8% of the time, Pallas kernels for 0%

commit v1 on v0

--- a/solution.py
+++ b/solution.py
@@ -107,9 +107,16 @@
         alda_kernel, lax.axis_index("band") * row_count, row_count, 1
     )
     hartree = potential_split(density_share, cosine_table, sine_table, length)
-    potential = lax.all_gather(
-        hartree + kernel_rows[None] * density_share, "band", axis=2, tiled=True
-    )
+    array = hartree + kernel_rows[None] * density_share
+    ways, here = (lax.axis_size("band"), lax.axis_index("band"))
+    grown, reach = (array, 1)
+    while reach < ways:
+        theirs = lax.ppermute(grown, "band", [(d, d ^ reach) for d in range(ways)])
+        mine_first = jnp.concatenate([grown, theirs], axis=2)
+        theirs_first = jnp.concatenate([theirs, grown], axis=2)
+        grown = jnp.where(here & reach == 0, mine_first, theirs_first)
+        reach = 2 * reach
+    potential = grown
     weight = local_potential[None] - band_energies[:, None, None, None]
     fields = potential[:, None] * orbital_wide[None] + weight[None] * trial_wide
     trial_count = trial_vectors.shape[0]

time: 588 us -> 644 us (1.095)
  waiting for transfers between devices: 281 us -> 333 us
    ppermute x0 -> x3, waiting for transfers between devices: none -> 121 us  [per_device(): theirs = lax.ppermute(grown, 'band', [(d, d ^ reach) for d in range(ways)])]
    all_gather x1 -> x0, waiting for transfers between devices: 69.1 us -> none  [per_device(): lax.all_gather(hartree + kernel_rows[None] * density_share, 'band', axis=...]
    unnamed x32 -> x34, local copies, waits for them, and re-layouts: 34.5 us -> 34.5 us
  transfers between devices with their start and end apart: 7 -> 9, of which waited for: 7 -> 9; matrix products, arithmetic and copies ran while one was open for 8% -> 7% of each run, Pallas kernels for 0% -> 0%
where the time goes in v1:
time: 644 us; the launch traced here: 639 us
  waiting for transfers between devices  333 us (52%)
  local copies, waits for them, and re-layouts  108 us (17%)
  matrix products  102 us (16%)
  other arithmetic  35.6 us (6%)
  starting transfers between devices  26.6 us (4%)
  blocking collectives  17.8 us (3%)
  between operations  15.7 us (2%)
    ppermute x3, waiting for transfers between devices, per_device(): theirs = lax.ppermute(grown, 'band', [(d, d ^ reach) for d in range(ways)])  121 us
    dot_general x36, matrix products, contract(): return jnp.einsum(pattern, left_operand, right_operand, precision=highest)  98.2 us
    reduce_scatter x1, waiting for transfers between devices, per_device(): lax.psum_scatter(partial_value, 'band', scatter_dimension=2, tiled=True)  91.5 us
    all_to_all x2, waiting for transfers between devices, per_device(): lax.all_to_all(jnp.stack((real_part, imag_part)), 'grid', split_axis=2, c...  55.1 us
    unnamed x34, local copies, waits for them, and re-layouts  34.5 us
    all_to_all x1, waiting for transfers between devices, potential_split(): lax.all_to_all(jnp.stack((real_part, imag_part)), 'band', split_axis=3, c...  25.6 us
    all_to_all x1, waiting for transfers between devices, potential_split(): lax.all_to_all(jnp.stack((real_part, imag_part)), 'band', split_axis=4, c...  25.5 us
    all_to_all x1, blocking collectives, potential_split(): lax.all_to_all(jnp.stack((real_part, imag_part)), 'grid', split_axis=4, c...  17.8 us
  transfers between devices with their start and end apart: 9, of which 9 were waited for; matrix products, arithmetic and copies ran while one was open for 7% of the time, Pallas kernels for 0%

profile of v1, /device:TPU:0, one launch (start us, length us, event | category | flops | bytes accessed | tf_op | source)
XLA Modules:
  0.0 638.9 jit_solution(8089317602935812079)
XLA Ops:
  10.2 2.7 fusion.1
  13.0 91.5 %reduce-scatter.2.cloned.1.call-done = f32[2,32,16,128]{3,2,1,0:T(8,128)} async-done(((f32[2,32,128,128]{3,2,1,0:T(8,128)}), f32[2,32,16,128]{3,2,1,0:T(8,128)}) %reduce-scatter.2.cloned.1.call-update) | async-done | bytes 524304 | tf_op jit(solution)/shard_map/reduce_scatter | solution.py:104
  108.4 4.4 copy.166
  112.8 4.8 reshape.351
  117.6 4.6 all-to-all-start
  122.2 25.6 %all-to-all-done = f32[8,1,32768]{2,1,0:T(1,128)S(1)} async-done(((f32[8,1,32768]{2,1,0:T(1,128)}), f32[8,1,32768]{2,1,0:T(1,128)S(1)}, u32[]{:S(2)}, u32[]{:S(2)}) %all-to-all-start) | async-done | bytes 1048608 | tf_op jit(solution)/shard_map/all_to_all | solution.py:59
  149.4 4.3 reduce
  153.7 3.4 reshape.352
  157.1 2.6 copy.167
  160.4 3.5 convolution_multiply_fusion.1
  164.1 3.5 convolution_multiply_fusion
  167.6 14.0 %fusion.28 = f32[1,2,128,16,32]{2,4,3,1,0:T(8,128)S(1)} fusion(f32[128,2,32,16]{0,2,3,1:T(8,128)S(1)} %convolution_multiply_fusion.1, f32[2,32,16,128]{1,3,2,0:T(8,128)S(1)} %bitcast.275), kind=kOutput, calls=%fused_computation.47 | convolution fusion | flops 201687040 | bytes 1572864 | tf_op jit(solution)/shard_map/kxzy,yg->kgzx/dot_general | solution.py:19
  181.6 3.5 fusion.27
  185.2 4.4 copy.174
  189.6 4.8 reshape.353
  194.4 4.3 all-to-all-start.1
  198.9 14.2 %all-to-all-done.1 = f32[4,1,65536]{2,1,0:T(1,128)} async-done(((f32[4,1,65536]{2,1,0:T(1,128)}), f32[4,1,65536]{2,1,0:T(1,128)}, u32[]{:S(2)}, u32[]{:S(2)}) %all-to-all-start.1) | async-done | bytes 1048608 | tf_op jit(solution)/shard_map/all_to_all | solution.py:65
  213.2 4.6 reduce.1
  217.7 3.5 reshape.354
  221.2 4.9 copy.248
  226.1 2.3 fusion.317
  228.4 2.4 squeeze.38
  230.9 2.8 squeeze.39
  240.4 4.4 copy.176
  244.8 3.9 reshape.355
  248.7 17.8 %all_to_all.90 = f32[4,1,65536]{2,1,0:T(1,128)} all-to-all(f32[4,1,65536]{2,1,0:T(1,128)S(1)} %reshape.355), channel_id=1, replica_groups=mesh['band'=8,'grid'=4] {'grid'}, dimensions={0} | all-to-all | bytes 2097152 | tf_op jit(solution)/shard_map/all_to_all | solution.py:83
  266.5 4.6 reduce.2
  271.1 3.5 reshape.356
  274.5 4.9 copy.247
  279.4 2.3 fusion.316
  281.7 2.4 squeeze.40
  286.6 2.4 squeeze.41
  291.0 4.4 copy.178
  295.4 4.8 reshape.357
  300.3 4.1 all-to-all-start.3
  304.4 25.5 %all-to-all-done.3 = f32[8,1,32768]{2,1,0:T(1,128)S(1)} async-done(((f32[8,1,32768]{2,1,0:T(1,128)}), f32[8,1,32768]{2,1,0:T(1,128)S(1)}, u32[]{:S(2)}, u32[]{:S(2)}) %all-to-all-start.3) | async-done | bytes 1048608 | tf_op jit(solution)/shard_map/all_to_all | solution.py:89
  329.9 3.1 reduce.3
  333.0 3.4 reshape.358
  336.4 4.6 copy.179
  351.5 11.2 %collective-permute-done = f32[2,32,16,128]{3,2,1,0:T(8,128)S(1)} collective-permute-done((f32[2,32,16,128]{3,2,1,0:T(8,128)S(1)}, f32[2,32,16,128]{3,2,1,0:T(8,128)S(1)}, u32[]{:S(2)}, u32[]{:S(2)}) %collective-permute-start) | collective-permute-done | bytes 524320 | tf_op jit(solution)/shard_map/ppermute | solution.py:114
  363.0 22.9 %collective-permute-done.1 = f32[2,32,32,128]{3,2,1,0:T(8,128)S(1)} collective-permute-done((f32[2,32,32,128]{3,2,1,0:T(8,128)S(1)}, f32[2,32,32,128]{3,2,1,0:T(8,128)S(1)}, u32[]{:S(2)}, u32[]{:S(2)}) %collective-permute-start.1) | collective-permute-done | bytes 1048608 | tf_op jit(solution)/shard_map/ppermute | solution.py:114
  387.6 2.4 collective-permute-start.2
  392.6 87.0 %collective-permute-done.2 = f32[2,32,64,128]{3,2,1,0:T(8,128)} collective-permute-done((f32[2,32,64,128]{3,2,1,0:T(8,128)}, f32[2,32,64,128]{3,2,1,0:T(8,128)}, u32[]{:S(2)}, u32[]{:S(2)}) %collective-permute-start.2) | collective-permute-done | bytes 2097184 | tf_op jit(solution)/shard_map/ppermute | solution.py:114
  479.6 4.6 fusion.2
  495.1 2.7 add_bitcast_fusion.1
  498.3 4.4 copy.188
  502.7 4.9 all-to-all-start.4
  507.6 3.8 fusion.9
  520.2 2.5 add_bitcast_fusion
  523.1 4.4 copy.201
  527.6 28.2 %all-to-all-done.4 = f32[2,1,128,128,32]{3,4,1,0,2:T(8,128)} async-done(((f32[2,1,128,128,32]{3,4,1,0,2:T(8,128)}), f32[2,1,128,128,32]{3,4,1,0,2:T(8,128)}, u32[]{:S(2)}, u32[]{:S(2)}) %all-to-all-start.4) | async-done | bytes 4194336 | tf_op jit(solution)/shard_map/all_to_all | solution.py:132
  555.8 4.9 all-to-all-start.5
  560.6 2.7 copy.189
  564.3 3.6 fusion.93
  567.9 5.0 multiply_bitcast_fusion.3
  573.0 4.0 fusion.91
  577.0 4.9 multiply_bitcast_fusion.2
  581.9 27.0 %all-to-all-done.5 = f32[2,1,128,128,32]{3,4,1,0,2:T(8,128)} async-done(((f32[2,1,128,128,32]{3,4,1,0,2:T(8,128)}), f32[2,1,128,128,32]{3,4,1,0,2:T(8,128)}, u32[]{:S(2)}, u32[]{:S(2)}) %all-to-all-start.5) | async-done | bytes 4194336 | tf_op jit(solution)/shard_map/all_to_all | solution.py:132
  608.8 2.7 copy.202
  612.3 3.6 fusion.88
  616.1 3.8 fusion.86
  619.9 3.7 multiply_bitcast_fusion.1
  623.6 3.6 multiply_bitcast_fusion
  628.3 3.6 fusion.5
  (89 shorter events, 58.3 us)
Async XLA Ops:
  7.2 297.2 %copy-start = (f32[32,128,128]{2,1,0:T(8,128)S(1)}, f32[32,128,128]{2,1,0:T(8,128)}, u32[]{:S(2)}) copy-start(f32[32,128,128]{2,1,0:T(8,128)} %param.7) | copy-start | bytes 6291460
  7.2 97.3 %reduce-scatter.2.cloned.1.call-start = ((), (), s32[]{:S(2)}) async-start(), calls=%async_computation.7 | async-start | bytes 4718592 | tf_op jit(solution)/shard_map/reduce_scatter | solution.py:104
  7.2 3.0 copy-start.8
  8.9 1.3 copy-start.4
  117.6 30.2 %all-to-all-start = ((f32[8,1,32768]{2,1,0:T(1,128)}), f32[8,1,32768]{2,1,0:T(1,128)S(1)}, u32[]{:S(2)}, u32[]{:S(2)}) async-start(f32[8,1,32768]{2,1,0:T(1,128)} %reshape.351), calls=%async_computation.1 | async-start | bytes 2097152 | tf_op jit(solution)/shard_map/all_to_all | solution.py:59
  147.8 1.0 copy-start.11
  194.4 18.8 %all-to-all-start.1 = ((f32[4,1,65536]{2,1,0:T(1,128)}), f32[4,1,65536]{2,1,0:T(1,128)}, u32[]{:S(2)}, u32[]{:S(2)}) async-start(f32[4,1,65536]{2,1,0:T(1,128)} %reshape.353), calls=%async_computation.2 | async-start | bytes 2097152 | tf_op jit(solution)/shard_map/all_to_all | solution.py:65
  289.0 1.7 copy-start.12
  300.3 29.6 %all-to-all-start.3 = ((f32[8,1,32768]{2,1,0:T(1,128)}), f32[8,1,32768]{2,1,0:T(1,128)S(1)}, u32[]{:S(2)}, u32[]{:S(2)}) async-start(f32[8,1,32768]{2,1,0:T(1,128)} %reshape.357), calls=%async_computation.4 | async-start | bytes 2097152 | tf_op jit(solution)/shard_map/all_to_all | solution.py:89
  346.4 1.8 copy-start.10
  350.1 12.6 %collective-permute-start = (f32[2,32,16,128]{3,2,1,0:T(8,128)S(1)}, f32[2,32,16,128]{3,2,1,0:T(8,128)S(1)}, u32[]{:S(2)}, u32[]{:S(2)}) collective-permute-start(f32[2,32,16,128]{3,2,1,0:T(8,128)S(1)} %fusion.30), channel_id=1, source_target_pairs={{0,4},{4,0},{8,12},{12,8},{16,20},{20,16},{24,28},{28,24},{1,5},{5... | collective-permute-start | bytes 1572872 | tf_op jit(solution)/shard_map/ppermute | solution.py:114
  362.9 23.0 %collective-permute-start.1 = (f32[2,32,32,128]{3,2,1,0:T(8,128)S(1)}, f32[2,32,32,128]{3,2,1,0:T(8,128)S(1)}, u32[]{:S(2)}, u32[]{:S(2)}) collective-permute-start(f32[2,32,32,128]{3,2,1,0:T(8,128)S(1)} %maximum_select_fusion.2), channel_id=1, source_target_pairs={{0,8},{4,12},{8,0},{12,4},{16,24},{20,28},{24,16},{28,20},{1,9},{5... | collective-permute-start | bytes 3145736 | tf_op jit(solution)/shard_map/ppermute | solution.py:114
  387.6 92.0 %collective-permute-start.2 = (f32[2,32,64,128]{3,2,1,0:T(8,128)}, f32[2,32,64,128]{3,2,1,0:T(8,128)}, u32[]{:S(2)}, u32[]{:S(2)}) collective-permute-start(f32[2,32,64,128]{3,2,1,0:T(8,128)} %maximum_select_fusion.1), channel_id=1, source_target_pairs={{0,16},{4,20},{8,24},{12,28},{16,0},{20,4},{24,8},{28,12},{1,17},{... | collective-permute-start | bytes 6291464 | tf_op jit(solution)/shard_map/ppermute | solution.py:114
  390.7 88.9 %copy-start.5 = (f32[32,128,128]{2,1,0:T(8,128)S(1)}, f32[32,128,128]{2,1,0:T(8,128)}, u32[]{:S(2)}) copy-start(f32[32,128,128]{2,1,0:T(8,128)} %copy-done.4) | copy-start | bytes 6291460
  390.7 88.9 %copy-start.9 = (bf16[2,1,32,128,128]{4,3,2,1,0:T(8,128)(2,1)S(1)}, bf16[2,1,32,128,128]{4,3,2,1,0:T(8,128)(2,1)}, u32[]{:S(2)}) copy-start(bf16[2,1,32,128,128]{4,3,2,1,0:T(8,128)(2,1)} %param.6) | copy-start | bytes 6291460
  484.2 2.1 copy-start.2
  502.7 53.1 %all-to-all-start.4 = ((f32[2,1,128,128,32]{3,4,1,0,2:T(8,128)}), f32[2,1,128,128,32]{3,4,1,0,2:T(8,128)}, u32[]{:S(2)}, u32[]{:S(2)}) async-start(f32[2,1,128,128,32]{3,4,1,0,2:T(8,128)} %copy.188), calls=%async_computation.5 | async-start | bytes 8388608 | tf_op jit(solution)/shard_map/all_to_all | solution.py:132
  507.6 3.8 copy-start.3
  555.8 53.1 %all-to-all-start.5 = ((f32[2,1,128,128,32]{3,4,1,0,2:T(8,128)}), f32[2,1,128,128,32]{3,4,1,0,2:T(8,128)}, u32[]{:S(2)}, u32[]{:S(2)}) async-start(f32[2,1,128,128,32]{3,4,1,0,2:T(8,128)} %copy.201), calls=%async_computation.6 | async-start | bytes 8388608 | tf_op jit(solution)/shard_map/all_to_all | solution.py:132
  623.6 3.6 copy-start.6
  623.6 3.6 copy-start.7
  628.3 3.6 copy-start.1
Sparse Core Ops, SparseCore 0:
  13.1 91.3 reduce-scatter.1
